TPU v7x, 32 devices: a whole 2x2x4 slice. The times are simulated.
32 devices in a mesh: gz: 2 (over core), row: 4 (over y, x), col: 4 (over z).
Axes of the slice: x: 2, y: 2, z: 4, core: 2. Of those that a mesh axis runs over, the one named last changes fastest.
Arguments:
- rhs_sub: float32 [2, 3, 4, 96, 256], P('gz', None, 'row', 'col'), may hold values from -6 to 6
- rhs_top: float32 [2, 4, 96, 256], P(None, 'row', 'col'), may hold values from -6 to 6
- lower_sub: bfloat16 [2, 3, 4, 4, 256, 256], P('gz', None, 'row', 'col'), may hold values from -0.078125 to 0.078125
- lower_link: bfloat16 [2, 2, 4, 4, 256, 256], P('gz', None, 'row', 'col'), may hold values from -0.078125 to 0.078125
- lower_top: bfloat16 [1, 4, 4, 256, 256], P(None, 'row', 'col'), may hold values from -0.078125 to 0.078125
- inv_sub: bfloat16 [2, 3, 4, 256, 256], P('gz', None, 'row'), may hold values from -0.3 to 1.3
- inv_top: bfloat16 [2, 4, 256, 256], P(None, 'row'), may hold values from -0.3 to 1.3
- mask_sub: int32 [2, 3, 4, 4], P('gz', None, 'row', 'col'), may hold values 0 or 1
- mask_link: int32 [2, 2, 4, 4], P('gz', None, 'row', 'col'), may hold values 0 or 1
- mask_top: int32 [1, 4, 4], P(None, 'row', 'col'), may hold values 0 or 1
Outputs:
- sol_sub: float32 [2, 3, 4, 96, 256], P('gz', None, 'row', 'col')
- sol_top: float32 [2, 4, 96, 256], P(None, 'row', 'col')
All inputs are finite; a program needn't handle non-finite values. No bound on the sum of `mask_sub` or of `mask_link` or of `mask_top` on one device may be relied on, other than what follows from the above.
Results may differ from a plain program's by a relative error of at most 0.02.
Values may be sent and summed in bfloat16 or wider, within the bound.
A program may use at most 64 MiB of HBM per device.

v0:
```python
import jax
import jax.numpy as jnp
from jax import lax
from jax.sharding import PartitionSpec as P


def forward_terms(column_vectors, blocks, pattern):
    product = jnp.einsum(
        "jnb,ijbd->ijnd", column_vectors, blocks, preferred_element_type=jnp.float32
    )
    return jnp.sum(product * pattern.astype(jnp.float32)[:, :, None, None], axis=1)


def backward_terms(row_vectors, blocks, pattern):
    product = jnp.einsum("knd,kjbd->kjnb", row_vectors, blocks, preferred_element_type=jnp.float32)
    return jnp.sum(product * pattern.astype(jnp.float32)[:, :, None, None], axis=0)


def inverse_rows(residual, inverse):
    return jnp.einsum(
        "inb,ibd->ind", residual.astype(jnp.bfloat16), inverse, preferred_element_type=jnp.float32
    )


def inverse_cols(residual, inverse):
    return jnp.einsum(
        "ind,ibd->inb", residual.astype(jnp.bfloat16), inverse, preferred_element_type=jnp.float32
    )


def own_share(values, share_cols):
    return lax.dynamic_slice_in_dim(values, lax.axis_index("col") * share_cols, share_cols, 1)


def level_solve(partial_sum, rhs_local, inverse, gate_value, across_groups):
    share_cols = rhs_local.shape[1]
    col_index = lax.axis_index("col")
    placed = lax.dynamic_update_slice_in_dim(
        jnp.zeros_like(partial_sum), rhs_local * gate_value, col_index * share_cols, 1
    )
    residual = lax.psum((placed - partial_sum).astype(jnp.bfloat16), "col").astype(jnp.float32)
    if across_groups:
        residual = lax.psum(residual.astype(jnp.bfloat16), "gz").astype(jnp.float32)
    result = inverse_rows(residual, inverse)
    return result


def column_vectors(rounded, col_blocks):
    col_index = lax.axis_index("col")
    every_block = lax.all_gather(rounded, "row", axis=0, tiled=True)
    result = lax.dynamic_slice_in_dim(every_block, col_index * col_blocks, col_blocks, 0)
    return result


def back_solve(back_part, solved_rows, inverse, share_cols):
    row_blocks = solved_rows.shape[0]
    summed = lax.psum(back_part.astype(jnp.bfloat16), "row").astype(jnp.float32)
    every_block = lax.all_gather(summed.astype(jnp.bfloat16), "col", axis=0, tiled=True).astype(
        summed.dtype
    )
    own_rows = lax.dynamic_slice_in_dim(
        every_block, lax.axis_index("row") * row_blocks, row_blocks, 0
    )
    answer = inverse_cols(solved_rows - own_rows, inverse)
    share = own_share(answer, share_cols)
    half = answer.astype(jnp.bfloat16)
    return (share, half)


def per_device(
    rhs_sub,
    rhs_top,
    lower_sub,
    lower_link,
    lower_top,
    inv_sub,
    inv_top,
    mask_sub,
    mask_link,
    mask_top,
):
    sub_levels = inv_sub.shape[1]
    top_levels = inv_top.shape[0]
    col_blocks = lower_top.shape[2]
    share_cols = rhs_top.shape[2]
    group_gate = (lax.axis_index("gz") == 0).astype(jnp.float32)
    unit_gate = jnp.float32(1.0)
    row_shape = (inv_top.shape[1], share_cols * lax.axis_size("col"), inv_top.shape[-1])
    column_shape = (col_blocks, row_shape[1], row_shape[2])
    sub_solved = []
    sub_columns = []
    for tier_index in range(sub_levels):
        partial_sum = jnp.zeros(row_shape, jnp.float32)
        for earlier in range(tier_index):
            pair_index = tier_index * (tier_index - 1) // 2 + earlier
            partial_sum = partial_sum + forward_terms(
                sub_columns[earlier], lower_sub[0, pair_index], mask_sub[0, pair_index]
            )
        solved = level_solve(
            partial_sum, rhs_sub[0, tier_index], inv_sub[0, tier_index], unit_gate, False
        )
        sub_solved.append(solved)
        sub_columns.append(column_vectors(solved.astype(jnp.bfloat16), col_blocks))
    top_solved = []
    top_columns = []
    for top_level in range(top_levels):
        partial_sum = forward_terms(
            sub_columns[sub_levels - 1], lower_link[0, top_level], mask_link[0, top_level]
        )
        for earlier in range(top_level):
            pair_index = top_level * (top_level - 1) // 2 + earlier
            partial_sum = partial_sum + group_gate * forward_terms(
                top_columns[earlier], lower_top[pair_index], mask_top[pair_index]
            )
        solved = level_solve(partial_sum, rhs_top[top_level], inv_top[top_level], group_gate, True)
        top_solved.append(solved)
        if top_level + 1 < top_levels:
            top_columns.append(column_vectors(solved.astype(jnp.bfloat16), col_blocks))
    top_share = [None] * top_levels
    top_half = [None] * top_levels
    for top_level in reversed(range(top_levels)):
        if top_level + 1 == top_levels:
            answer = inverse_cols(top_solved[top_level], inv_top[top_level])
            share = own_share(answer, share_cols)
            half = answer.astype(jnp.bfloat16)
        else:
            later_level = 1
            pair_index = later_level * (later_level - 1) // 2 + top_level
            back_part = backward_terms(
                top_half[later_level], lower_top[pair_index], mask_top[pair_index]
            )
            share, half = back_solve(
                back_part, top_solved[top_level], inv_top[top_level], share_cols
            )
        top_share[top_level] = share
        top_half[top_level] = half
    sub_share = [None] * sub_levels
    sub_half = [None] * sub_levels
    for tier_index in reversed(range(sub_levels)):
        back_part = jnp.zeros(column_shape, jnp.float32)
        for later_level in range(tier_index + 1, sub_levels):
            pair_index = later_level * (later_level - 1) // 2 + tier_index
            back_part = back_part + backward_terms(
                sub_half[later_level], lower_sub[0, pair_index], mask_sub[0, pair_index]
            )
        if tier_index == sub_levels - 1:
            for top_level in range(top_levels):
                back_part = back_part + backward_terms(
                    top_half[top_level], lower_link[0, top_level], mask_link[0, top_level]
                )
        share, half = back_solve(
            back_part, sub_solved[tier_index], inv_sub[0, tier_index], share_cols
        )
        sub_share[tier_index] = share
        sub_half[tier_index] = half
    sol_sub = jnp.stack(sub_share)[None]
    sol_top = jnp.stack(top_share)
    return (sol_sub, sol_top)


def solution(mesh):
    return jax.shard_map(
        per_device,
        mesh=mesh,
        in_specs=(
            P("gz", None, "row", "col", None),
            P(None, "row", "col", None),
            P("gz", None, "row", "col", None, None),
            P("gz", None, "row", "col", None, None),
            P(None, "row", "col", None, None),
            P("gz", None, "row", None, None),
            P(None, "row", None, None),
            P("gz", None, "row", "col"),
            P("gz", None, "row", "col"),
            P(None, "row", "col"),
        ),
        out_specs=(P("gz", None, "row", "col", None), P(None, "row", "col", None)),
        check_vma=False,
    )
```

profile of v0, /device:TPU:0, one launch (start us, length us, event | category | flops | bytes accessed | tf_op | source)
XLA Modules:
  0.0 261.6 jit_solution(2911516491720442301)
XLA Ops:
  0.7 0.8 bitcast_dynamic-update-slice_fusion.4
  1.5 21.3 %psum.77 = bf16[96,256]{1,0:T(8,128)(2,1)S(1)} all-reduce(bf16[96,256]{1,0:T(8,128)(2,1)S(1)} %convert_bitcast_fusion), channel_id=1, replica_groups=mesh['gz'=2,'row'=4,'col'=4] {'col'}, use_global_device_ids=true, to_apply=%region_0.0 | all-reduce | flops 24576 | bytes 98304 | tf_op jit(solution)/shard_map/psum | solution.py:41
  22.9 8.7 %all-gather = bf16[384,256]{1,0:T(8,128)(2,1)S(1)} all-gather(bf16[96,256]{1,0:T(8,128)(2,1)S(1)} %get-tuple-element.7), channel_id=2, replica_groups=mesh['gz'=2,'row'=4,'col'=4] {'row'}, dimensions={0}, use_global_device_ids=true | all-gather | bytes 245760 | tf_op jit(solution)/shard_map/all_gather | solution.py:50
  31.7 0.9 copy-done.5
  32.6 0.6 copy-done.7
  33.2 0.6 fusion.123
  34.6 16.1 %psum.78 = bf16[96,256]{1,0:T(8,128)(2,1)S(1)} all-reduce(bf16[96,256]{1,0:T(8,128)(2,1)S(1)} %fusion.26), channel_id=1, replica_groups=mesh['gz'=2,'row'=4,'col'=4] {'col'}, use_global_device_ids=true, to_apply=%region_1.0 | all-reduce | flops 24576 | bytes 98304 | tf_op jit(solution)/shard_map/psum | solution.py:41
  50.9 8.7 %all-gather.1 = bf16[384,256]{1,0:T(8,128)(2,1)S(1)} all-gather(bf16[96,256]{1,0:T(8,128)(2,1)S(1)} %get-tuple-element.9), channel_id=3, replica_groups=mesh['gz'=2,'row'=4,'col'=4] {'row'}, dimensions={0}, use_global_device_ids=true | all-gather | bytes 245760 | tf_op jit(solution)/shard_map/all_gather | solution.py:50
  61.2 18.0 %psum.79 = bf16[96,256]{1,0:T(8,128)(2,1)S(1)} all-reduce(bf16[96,256]{1,0:T(8,128)(2,1)S(1)} %fusion.27), channel_id=1, replica_groups=mesh['gz'=2,'row'=4,'col'=4] {'col'}, use_global_device_ids=true, to_apply=%region_2.0 | all-reduce | flops 24576 | bytes 98304 | tf_op jit(solution)/shard_map/psum | solution.py:41
  79.4 7.9 %all-gather.2 = bf16[384,256]{1,0:T(8,128)(2,1)S(1)} all-gather(bf16[96,256]{1,0:T(8,128)(2,1)S(1)} %get-tuple-element.11), channel_id=4, replica_groups=mesh['gz'=2,'row'=4,'col'=4] {'row'}, dimensions={0}, use_global_device_ids=true | all-gather | bytes 245760 | tf_op jit(solution)/shard_map/all_gather | solution.py:50
  87.2 0.8 copy-done.6
  88.0 0.6 copy-done.8
  88.7 0.6 fusion.122
  90.2 16.1 %psum.80 = bf16[1,96,256]{2,1,0:T(8,128)(2,1)S(1)} all-reduce(bf16[1,96,256]{2,1,0:T(8,128)(2,1)S(1)} %fusion.17), channel_id=1, replica_groups=mesh['gz'=2,'row'=4,'col'=4] {'col'}, use_global_device_ids=true, to_apply=%region_3.0 | all-reduce | flops 24576 | bytes 98304 | tf_op jit(solution)/shard_map/psum | solution.py:41
  106.3 3.5 %psum.81 = bf16[96,256]{1,0:T(8,128)(2,1)S(1)} all-reduce(bf16[96,256]{1,0:T(8,128)(2,1)S(1)} %bitcast.253), channel_id=1, replica_groups=mesh['gz'=2,'row'=4,'col'=4] {'gz'}, use_global_device_ids=true, to_apply=%region_4.0 | all-reduce | flops 24576 | bytes 98304 | tf_op jit(solution)/shard_map/psum | solution.py:43
  110.0 8.7 %all-gather.3 = bf16[384,256]{1,0:T(8,128)(2,1)S(1)} all-gather(bf16[96,256]{1,0:T(8,128)(2,1)S(1)} %get-tuple-element.13), channel_id=5, replica_groups=mesh['gz'=2,'row'=4,'col'=4] {'row'}, dimensions={0}, use_global_device_ids=true | all-gather | bytes 245760 | tf_op jit(solution)/shard_map/all_gather | solution.py:50
  120.4 18.0 %psum.82 = bf16[1,96,256]{2,1,0:T(8,128)(2,1)S(1)} all-reduce(bf16[1,96,256]{2,1,0:T(8,128)(2,1)S(1)} %fusion.16), channel_id=1, replica_groups=mesh['gz'=2,'row'=4,'col'=4] {'col'}, use_global_device_ids=true, to_apply=%region_5.0 | all-reduce | flops 24576 | bytes 98304 | tf_op jit(solution)/shard_map/psum | solution.py:41
  138.4 3.5 %psum.83 = bf16[96,256]{1,0:T(8,128)(2,1)S(1)} all-reduce(bf16[96,256]{1,0:T(8,128)(2,1)S(1)} %bitcast.254), channel_id=1, replica_groups=mesh['gz'=2,'row'=4,'col'=4] {'gz'}, use_global_device_ids=true, to_apply=%region_6.0 | all-reduce | flops 24576 | bytes 98304 | tf_op jit(solution)/shard_map/psum | solution.py:43
  142.0 0.3 fusion.21
  142.5 15.8 %psum.84 = bf16[1,96,256]{2,1,0:T(8,128)(2,1)S(1)} all-reduce(bf16[1,96,256]{2,1,0:T(8,128)(2,1)S(1)} %fusion.23), channel_id=1, replica_groups=mesh['gz'=2,'row'=4,'col'=4] {'row'}, use_global_device_ids=true, to_apply=%region_7.0 | all-reduce | flops 24576 | bytes 98304 | tf_op jit(solution)/shard_map/psum | solution.py:57
  158.3 13.7 %all_gather.28 = bf16[4,96,256]{2,1,0:T(8,128)(2,1)S(1)} all-gather(bf16[1,96,256]{2,1,0:T(8,128)(2,1)S(1)} %psum.84), channel_id=1, replica_groups=mesh['gz'=2,'row'=4,'col'=4] {'col'}, dimensions={0}, use_global_device_ids=true | all-gather | bytes 245760 | tf_op jit(solution)/shard_map/all_gather | solution.py:58
  172.2 0.6 pad_maximum_fusion
  173.0 0.2 fusion.24
  173.2 14.7 %psum.85 = bf16[1,96,256]{2,1,0:T(8,128)(2,1)S(1)} all-reduce(bf16[1,96,256]{2,1,0:T(8,128)(2,1)S(1)} %fusion.24), channel_id=1, replica_groups=mesh['gz'=2,'row'=4,'col'=4] {'row'}, use_global_device_ids=true, to_apply=%region_8.0 | all-reduce | flops 24576 | bytes 98304 | tf_op jit(solution)/shard_map/psum | solution.py:57
  187.9 13.6 %all_gather.29 = bf16[4,96,256]{2,1,0:T(8,128)(2,1)S(1)} all-gather(bf16[1,96,256]{2,1,0:T(8,128)(2,1)S(1)} %psum.85), channel_id=1, replica_groups=mesh['gz'=2,'row'=4,'col'=4] {'col'}, dimensions={0}, use_global_device_ids=true | all-gather | bytes 245760 | tf_op jit(solution)/shard_map/all_gather | solution.py:58
  201.7 0.2 fusion.22
  201.9 15.7 %psum.86 = bf16[1,96,256]{2,1,0:T(8,128)(2,1)S(1)} all-reduce(bf16[1,96,256]{2,1,0:T(8,128)(2,1)S(1)} %fusion.22), channel_id=1, replica_groups=mesh['gz'=2,'row'=4,'col'=4] {'row'}, use_global_device_ids=true, to_apply=%region_9.0 | all-reduce | flops 24576 | bytes 98304 | tf_op jit(solution)/shard_map/psum | solution.py:57
  217.6 13.8 %all_gather.30 = bf16[4,96,256]{2,1,0:T(8,128)(2,1)S(1)} all-gather(bf16[1,96,256]{2,1,0:T(8,128)(2,1)S(1)} %psum.86), channel_id=1, replica_groups=mesh['gz'=2,'row'=4,'col'=4] {'col'}, dimensions={0}, use_global_device_ids=true | all-gather | bytes 245760 | tf_op jit(solution)/shard_map/all_gather | solution.py:58
  231.5 0.2 convolution_multiply_fusion
  232.0 15.2 %psum.87 = bf16[1,96,256]{2,1,0:T(8,128)(2,1)S(1)} all-reduce(bf16[1,96,256]{2,1,0:T(8,128)(2,1)S(1)} %fusion.25), channel_id=1, replica_groups=mesh['gz'=2,'row'=4,'col'=4] {'row'}, use_global_device_ids=true, to_apply=%region_10.0 | all-reduce | flops 24576 | bytes 98304 | tf_op jit(solution)/shard_map/psum | solution.py:57
  247.2 13.6 %all_gather.31 = bf16[4,96,256]{2,1,0:T(8,128)(2,1)S(1)} all-gather(bf16[1,96,256]{2,1,0:T(8,128)(2,1)S(1)} %psum.87), channel_id=1, replica_groups=mesh['gz'=2,'row'=4,'col'=4] {'col'}, dimensions={0}, use_global_device_ids=true | all-gather | bytes 245760 | tf_op jit(solution)/shard_map/all_gather | solution.py:58
  261.0 0.6 maximum_bitcast_fusion
  (46 shorter events, 3.0 us)
Async XLA Ops:
  0.6 118.7 %copy-start = (bf16[1,1,1,256,256]{4,3,2,1,0:T(8,128)(2,1)S(1)}, bf16[1,1,1,256,256]{4,3,2,1,0:T(8,128)(2,1)}, u32[]{:S(2)}) copy-start(bf16[1,1,1,256,256]{4,3,2,1,0:T(8,128)(2,1)} %param.14) | copy-start | bytes 393220
  0.6 22.1 %copy-start.2 = (bf16[1,3,1,256,256]{4,3,2,1,0:T(8,128)(2,1)S(1)}, bf16[1,3,1,256,256]{4,3,2,1,0:T(8,128)(2,1)}, u32[]{:S(2)}) copy-start(bf16[1,3,1,256,256]{4,3,2,1,0:T(8,128)(2,1)} %param.15) | copy-start | bytes 1179652
  22.8 11.7 %copy-start.1 = (bf16[1,3,1,1,256,256]{5,4,3,2,1,0:T(8,128)(2,1)S(1)}, bf16[1,3,1,1,256,256]{5,4,3,2,1,0:T(8,128)(2,1)}, u32[]{:S(2)}) copy-start(bf16[1,3,1,1,256,256]{5,4,3,2,1,0:T(8,128)(2,1)} %param.12) | copy-start | bytes 1179652
  31.7 0.9 copy-start.5
  32.6 0.7 copy-start.7
  79.4 10.6 %copy-start.3 = (bf16[1,2,1,1,256,256]{5,4,3,2,1,0:T(8,128)(2,1)S(1)}, bf16[1,2,1,1,256,256]{5,4,3,2,1,0:T(8,128)(2,1)}, u32[]{:S(2)}) copy-start(bf16[1,2,1,1,256,256]{5,4,3,2,1,0:T(8,128)(2,1)} %param.13) | copy-start | bytes 786436
  87.2 0.8 copy-start.6
  88.0 0.7 copy-start.8
  90.0 19.8 %copy-start.4 = (bf16[2,1,256,256]{3,2,1,0:T(8,128)(2,1)S(1)}, bf16[2,1,256,256]{3,2,1,0:T(8,128)(2,1)}, u32[]{:S(2)}) copy-start(bf16[2,1,256,256]{3,2,1,0:T(8,128)(2,1)} %param.16) | copy-start | bytes 786436
where the time goes:
time: 262 us
  blocking collectives  247 us (94%)
  local copies, waits for them, and re-layouts  5.17 us (2%)
  between operations  4.84 us (2%)
  matrix products  3.7 us (1%)
    psum x5, blocking collectives, level_solve(): lax.psum((placed - partial_sum).astype(jnp.bfloat16), 'col')  89.5 us
    psum x4, blocking collectives, back_solve(): summed = lax.psum(back_part.astype(jnp.bfloat16), 'row').astype(jnp.float32)  61.4 us
    all_gather x4, blocking collectives, back_solve(): lax.all_gather(summed.astype(jnp.bfloat16), 'col', axis=0, tiled=True)  54.6 us
    all_gather x4, blocking collectives, column_vectors(): every_block = lax.all_gather(rounded, 'row', axis=0, tiled=True)  34 us
    psum x2, blocking collectives, level_solve(): residual = lax.psum(residual.astype(jnp.bfloat16), 'gz').astype(jnp.float32)  7.06 us

commit v1 on v0

--- a/solution.py
+++ b/solution.py
@@ -1,6 +1,8 @@
 import jax
 import jax.numpy as jnp
 from jax import lax
+from jax.experimental import pallas as pl
+from jax.experimental.pallas import tpu as pltpu
 from jax.sharding import PartitionSpec as P
 
 
@@ -158,9 +160,294 @@
     return (sol_sub, sol_top)
 
 
+MESH = pl.DeviceIdType.MESH
+
+
+def pair_of(later, earlier):
+    return later * (later - 1) // 2 + earlier
+
+
+def dot_nn(x, w):
+    return lax.dot_general(x, w, (((1,), (0,)), ((), ())), preferred_element_type=jnp.float32)
+
+
+def dot_nt(x, w):
+    return lax.dot_general(x, w, (((1,), (1,)), ((), ())), preferred_element_type=jnp.float32)
+
+
+def fused_kernel(
+    rhs_sub,
+    rhs_top,
+    lower_sub,
+    lower_link,
+    lower_top,
+    inv_sub,
+    inv_top,
+    mask_sub,
+    mask_link,
+    mask_top,
+    sol_sub,
+    sol_top,
+    lm,
+    solved,
+    hout,
+    hin,
+    pout,
+    pin,
+    xout,
+    xin,
+    ans,
+    qout,
+    qin,
+    h_send,
+    h_recv,
+    p_send,
+    p_recv,
+    x_send,
+    x_recv,
+    a_send,
+    a_recv,
+    q_send,
+    q_recv,
+):
+    subl, topl = rhs_sub.shape[1], rhs_top.shape[0]
+    pairs, tpairs = lower_sub.shape[1], lower_top.shape[0]
+    levels = subl + topl
+    n, share, width = hin.shape[1], hin.shape[2], hin.shape[3]
+    g, i, j = lax.axis_index("gz"), lax.axis_index("row"), lax.axis_index("col")
+    pending = []
+
+    def put(src, dst, send_sem, recv_sem, where, remote=None):
+        copy = pltpu.make_async_remote_copy(
+            src_ref=src,
+            dst_ref=dst,
+            send_sem=send_sem,
+            recv_sem=recv_sem,
+            device_id=where,
+            device_id_type=MESH,
+        )
+        pending.append((copy, remote))
+        if remote is None:
+            copy.start()
+            return
+
+        @pl.when(remote)
+        def _():
+            copy.start()
+
+        @pl.when(jnp.logical_not(remote))
+        def _():
+            pltpu.make_async_copy(src, dst, recv_sem).start()
+
+    def arrived(dst, recv_sem):
+        pltpu.make_async_copy(dst, dst, recv_sem).wait()
+
+    def wide(ref):
+        return ref[...].astype(jnp.float32).reshape(n * share, width).astype(jnp.bfloat16)
+
+    def inverse(level):
+        return inv_sub[0, level, 0] if level < subl else inv_top[level - subl, 0]
+
+    def rhs(level):
+        return rhs_sub[0, level, 0] if level < subl else rhs_top[level - subl, 0]
+
+    for unit in range(pairs + topl + tpairs):
+        if unit < pairs:
+            block, mask = lower_sub[0, unit, 0, 0], mask_sub[0, unit, 0, 0]
+        elif unit < pairs + topl:
+            block, mask = lower_link[0, unit - pairs, 0, 0], mask_link[0, unit - pairs, 0, 0]
+        else:
+            at = unit - pairs - topl
+            block, mask = lower_top[at, 0, 0], mask_top[at, 0, 0]
+        lm[unit] = (block.astype(jnp.float32) * mask.astype(jnp.float32)).astype(jnp.bfloat16)
+
+    def earlier_units(level):
+        if level < subl:
+            return [(b, pair_of(level, b)) for b in range(level)]
+        t = level - subl
+        return [(subl - 1, pairs + t)] + [
+            (subl + b, pairs + topl + pair_of(t, b)) for b in range(t)
+        ]
+
+    def later_units(level):
+        if level >= subl:
+            t = level - subl
+            return [(subl + a, pairs + topl + pair_of(a, t)) for a in range(t + 1, topl)]
+        found = [(a, pair_of(a, level)) for a in range(level + 1, subl)]
+        if level == subl - 1:
+            found += [(subl + t, pairs + t) for t in range(topl)]
+        return found
+
+    columns = {}
+    for level in range(levels):
+        residual = rhs(level)
+        if level > 0:
+            last = level - 1
+            for c in range(n):
+                arrived(hin.at[last, c], h_recv.at[last, c])
+            columns[last] = wide(hin.at[last])
+            part = None
+            for b, unit in earlier_units(level):
+                term = dot_nn(columns[b], lm[unit])
+                part = term if part is None else part + term
+            pout[level - 1] = part.reshape(n, share, width).astype(jnp.bfloat16)
+            for d in range(1, n):
+                c = lax.rem(j + d, n)
+                put(
+                    pout.at[level - 1, c],
+                    pin.at[level - 1, j],
+                    p_send.at[level - 1, d],
+                    p_recv.at[level - 1, j],
+                    {"col": c},
+                )
+            if level == subl:
+                for t in range(topl):
+                    term = part if t == 0 else dot_nn(columns[subl - 1], lm[pairs + t])
+                    xout[:, t] = term.reshape(n, share, width).astype(jnp.bfloat16)
+                for d in range(n):
+                    c = lax.rem(j + d, n)
+                    put(
+                        xout.at[c],
+                        xin.at[j],
+                        x_send.at[d],
+                        x_recv.at[j],
+                        {"gz": 1 - g, "col": c},
+                    )
+            residual = residual - pout[level - 1, j].astype(jnp.float32)
+            for d in range(1, n):
+                c = lax.rem(j + d, n)
+                arrived(pin.at[level - 1, c], p_recv.at[level - 1, c])
+                residual = residual - pin[level - 1, c].astype(jnp.float32)
+            if level >= subl:
+                for c in range(n):
+                    if level == subl:
+                        arrived(xin.at[c], x_recv.at[c])
+                    residual = residual - xin[c, level - subl].astype(jnp.float32)
+        result = dot_nn(residual.astype(jnp.bfloat16), inverse(level))
+        solved[level] = result
+        if level + 1 < levels:
+            hout[level] = result.astype(jnp.bfloat16)
+            for d in range(n):
+                put(
+                    hout.at[level],
+                    hin.at[level, j],
+                    h_send.at[level, d],
+                    h_recv.at[level, j],
+                    {"row": lax.rem(i + d, n), "col": i},
+                    None if d else i != j,
+                )
+
+    rows = {}
+    for level in reversed(range(levels)):
+        total = solved[level]
+        if level + 1 < levels:
+            last = level + 1
+            for d in range(1, n):
+                c = lax.rem(j + d, n)
+                arrived(ans.at[last, c], a_recv.at[last, c])
+            rows[last] = wide(ans.at[last])
+            part = None
+            for a, unit in later_units(level):
+                term = dot_nt(rows[a], lm[unit])
+                part = term if part is None else part + term
+            qout[level] = part.reshape(n, share, width).astype(jnp.bfloat16)
+            for d in range(n):
+                c = lax.rem(j + d, n)
+                put(
+                    qout.at[level, c],
+                    qin.at[level, i],
+                    q_send.at[level, d],
+                    q_recv.at[level, i],
+                    {"row": j, "col": c},
+                    None if d else i != j,
+                )
+            for k in range(n):
+                arrived(qin.at[level, k], q_recv.at[level, k])
+                total = total - qin[level, k].astype(jnp.float32)
+        result = dot_nt(total.astype(jnp.bfloat16), inverse(level))
+        if level < subl:
+            sol_sub[0, level, 0] = result
+        else:
+            sol_top[level - subl, 0] = result
+        if level > 0:
+            ans[level, j] = result.astype(jnp.bfloat16)
+            for d in range(1, n):
+                put(
+                    ans.at[level, j],
+                    ans.at[level, j],
+                    a_send.at[level, d],
+                    a_recv.at[level, j],
+                    {"col": lax.rem(j + d, n)},
+                )
+
+    for copy, remote in pending:
+        if remote is None:
+            copy.wait_send()
+        else:
+
+            @pl.when(remote)
+            def _():
+                copy.wait_send()
+
+
+def fused_device(*args):
+    rhs_sub, rhs_top, lower_sub, lower_link, lower_top = args[:5]
+    levels = rhs_sub.shape[1] + rhs_top.shape[0]
+    topl = rhs_top.shape[0]
+    share, width = rhs_top.shape[2:]
+    n = lax.axis_size("col")
+    units = lower_sub.shape[1] + lower_link.shape[1] + lower_top.shape[0]
+    half, dma = jnp.bfloat16, pltpu.SemaphoreType.DMA
+    vmem = pl.BlockSpec(memory_space=pltpu.VMEM)
+    smem = pl.BlockSpec(memory_space=pltpu.SMEM)
+    vectors = pltpu.VMEM((levels, n, share, width), half)
+    return pl.pallas_call(
+        fused_kernel,
+        out_shape=(
+            jax.ShapeDtypeStruct(rhs_sub.shape, jnp.float32),
+            jax.ShapeDtypeStruct(rhs_top.shape, jnp.float32),
+        ),
+        in_specs=[vmem] * 7 + [smem] * 3,
+        out_specs=(vmem, vmem),
+        scratch_shapes=[
+            pltpu.VMEM((units, width, width), half),
+            pltpu.VMEM((levels, share, width), jnp.float32),
+            pltpu.VMEM((levels, share, width), half),
+            vectors,
+            vectors,
+            vectors,
+            pltpu.VMEM((n, topl, share, width), half),
+            pltpu.VMEM((n, topl, share, width), half),
+            vectors,
+            vectors,
+            vectors,
+            dma((levels, n)),
+            dma((levels, n)),
+            dma((levels, n)),
+            dma((levels, n)),
+            dma((n,)),
+            dma((n,)),
+            dma((levels, n)),
+            dma((levels, n)),
+            dma((levels, n)),
+            dma((levels, n)),
+        ],
+        compiler_params=pltpu.CompilerParams(has_side_effects=True),
+    )(*args)
+
+
+def choose(*args):
+    rhs_top, lower_top = args[1], args[4]
+    one_each = lower_top.shape[1] == 1 and lower_top.shape[2] == 1
+    square = lax.axis_size("row") == lax.axis_size("col") and lax.axis_size("gz") == 2
+    if one_each and square and rhs_top.shape[2] % 8 == 0 and rhs_top.shape[3] % 128 == 0:
+        return fused_device(*args)
+    return per_device(*args)
+
+
 def solution(mesh):
     return jax.shard_map(
-        per_device,
+        choose,
         mesh=mesh,
         in_specs=(
             P("gz", None, "row", "col", None),

time: 262 us -> 86 us (0.33)
  blocking collectives: 247 us -> 0 us
  Pallas kernels: 0 us -> 81 us
  matrix products: 3.7 us -> 0 us
  between operations: 4.84 us -> 1.33 us
    psum x11 -> x0, blocking collectives: 158 us -> none  [the longest x5 89.5 us: level_solve(): lax.psum((placed - partial_sum).astype(jnp.bfloat16), 'col')]
    all_gather x8 -> x0, blocking collectives: 88.6 us -> none  [the longest x4 54.6 us: back_solve(): lax.all_gather(summed.astype(jnp.bfloat16), 'col', axis=0, tiled=True)]
    pallas_call x0 -> x1, Pallas kernels: none -> 81 us  [fused_device(): pl.pallas_call(fused_kernel, out_shape=(jax.ShapeDtypeStruct(rhs_sub.shap...]
    dot_general x21 -> x0, matrix products: 3.7 us -> none  [the longest x6 1.21 us: backward_terms(): jnp.einsum('knd,kjbd->kjnb', row_vectors, blocks, preferred_element_type=...]
where the time goes in v1:
time: 86 us; the launch traced here: 85.8 us
  Pallas kernels  81 us (94%)
  local copies, waits for them, and re-layouts  3.46 us (4%)
  between operations  1.33 us (2%)
    pallas_call x1, Pallas kernels, fused_device(): pl.pallas_call(fused_kernel, out_shape=(jax.ShapeDtypeStruct(rhs_sub.shap...  81 us
    unnamed x10, local copies, waits for them, and re-layouts  3.46 us

profile of v1, /device:TPU:0, one launch (start us, length us, event | category | flops | bytes accessed | tf_op | source)
XLA Modules:
  0.0 85.8 jit_solution(12788911923990591946)
XLA Ops:
  0.6 0.0 copy-start.2
  1.3 0.0 copy-done.2
  1.3 0.0 copy-start.1
  1.3 0.6 copy.13.mask_link
  2.0 0.0 copy-done.1
  2.0 0.6 copy.12.mask_sub
  2.6 81.0 %shard_map.113 = (f32[1,3,1,24,256]{4,3,2,1,0:T(8,128)}, f32[2,1,24,256]{3,2,1,0:T(8,128)}) custom-call(f32[1,3,1,24,256]{4,3,2,1,0:T(8,128)} %rhs_sub.1, f32[2,1,24,256]{3,2,1,0:T(8,128)} %rhs_top.1, bf16[1,3,1,1,256,256]{5,4,3,2,1,0:T(8,128)(2,1)} %lower_sub.1, bf16[1,2,1,1,256,256]{5,4,3,2,1,0:T(8,128)(2,1)} %lower_link.1, ...), custom_call_target="tpu_custom_call" | custom-call | tf_op jit(solution)/shard_map/pallas_call | solution.py:404
  83.7 0.0 copy-start
  83.7 1.5 %copy.17 = f32[1,3,1,24,256]{4,3,2,1,0:T(8,128)} copy(f32[1,3,1,24,256]{4,3,2,1,0:T(8,128)} %get-tuple-element.4) | data formatting | bytes 147456
  85.2 0.0 copy-done
  85.2 0.6 copy.18
Async XLA Ops:
  0.6 0.7 copy-start.2
  1.3 0.7 copy-start.1
  83.7 1.5 %copy-start = (f32[2,1,24,256]{3,2,1,0:T(8,128)S(1)}, f32[2,1,24,256]{3,2,1,0:T(8,128)}, u32[]{:S(2)}) copy-start(f32[2,1,24,256]{3,2,1,0:T(8,128)} %get-tuple-element.5) | copy-start | bytes 147460

commit v2 on v1

--- a/solution.py
+++ b/solution.py
@@ -183,13 +183,18 @@
     lower_top,
     inv_sub,
     inv_top,
-    mask_sub,
-    mask_link,
-    mask_top,
+    mask,
     sol_sub,
     sol_top,
     lm,
+    first,
     solved,
+    hout0,
+    hin0,
+    qout0,
+    qin0,
+    rin_sub,
+    rin_top,
     hout,
     hin,
     pout,
@@ -199,6 +204,10 @@
     ans,
     qout,
     qin,
+    back_out,
+    back_in,
+    r_send,
+    r_recv,
     h_send,
     h_recv,
     p_send,
@@ -209,15 +218,22 @@
     a_recv,
     q_send,
     q_recv,
+    b_send,
+    b_recv,
 ):
     subl, topl = rhs_sub.shape[1], rhs_top.shape[0]
     pairs, tpairs = lower_sub.shape[1], lower_top.shape[0]
     levels = subl + topl
-    n, share, width = hin.shape[1], hin.shape[2], hin.shape[3]
+    n, share, width = hin0.shape
+    mids, wide_share = hin.shape[1], hin.shape[2]
+    per_mid = n // mids
+    low = (n - mids) // 2
     g, i, j = lax.axis_index("gz"), lax.axis_index("row"), lax.axis_index("col")
+    is_mid = (j >= low) & (j < low + mids)
+    m = jnp.clip(j - low, 0, mids - 1)
     pending = []
 
-    def put(src, dst, send_sem, recv_sem, where, remote=None):
+    def put(src, dst, send_sem, recv_sem, where, remote=None, active=None):
         copy = pltpu.make_async_remote_copy(
             src_ref=src,
             dst_ref=dst,
@@ -226,40 +242,37 @@
             device_id=where,
             device_id_type=MESH,
         )
-        pending.append((copy, remote))
-        if remote is None:
+        goes = active
+        if remote is not None:
+            goes = remote if active is None else remote & active
+            stays = jnp.logical_not(remote)
+            stays = stays if active is None else stays & active
+
+            @pl.when(stays)
+            def _():
+                pltpu.make_async_copy(src, dst, recv_sem).start()
+
+        pending.append((copy, goes))
+        if goes is None:
             copy.start()
-            return
-
-        @pl.when(remote)
-        def _():
-            copy.start()
-
-        @pl.when(jnp.logical_not(remote))
-        def _():
-            pltpu.make_async_copy(src, dst, recv_sem).start()
+        else:
+
+            @pl.when(goes)
+            def _():
+                copy.start()
 
     def arrived(dst, recv_sem):
         pltpu.make_async_copy(dst, dst, recv_sem).wait()
 
-    def wide(ref):
-        return ref[...].astype(jnp.float32).reshape(n * share, width).astype(jnp.bfloat16)
-
     def inverse(level):
         return inv_sub[0, level, 0] if level < subl else inv_top[level - subl, 0]
 
     def rhs(level):
-        return rhs_sub[0, level, 0] if level < subl else rhs_top[level - subl, 0]
-
-    for unit in range(pairs + topl + tpairs):
-        if unit < pairs:
-            block, mask = lower_sub[0, unit, 0, 0], mask_sub[0, unit, 0, 0]
-        elif unit < pairs + topl:
-            block, mask = lower_link[0, unit - pairs, 0, 0], mask_link[0, unit - pairs, 0, 0]
+        if level < subl:
+            value = rin_sub[:, level - 1]
         else:
-            at = unit - pairs - topl
-            block, mask = lower_top[at, 0, 0], mask_top[at, 0, 0]
-        lm[unit] = (block.astype(jnp.float32) * mask.astype(jnp.float32)).astype(jnp.bfloat16)
+            value = rin_top[:, level - subl]
+        return value.reshape(wide_share, width)
 
     def earlier_units(level):
         if level < subl:
@@ -278,169 +291,273 @@
             found += [(subl + t, pairs + t) for t in range(topl)]
         return found
 
+    result = dot_nn(rhs_sub[0, 0, 0].astype(jnp.bfloat16), inverse(0))
+    first[...] = result
+    hout0[...] = result.astype(jnp.bfloat16)
+    for d in range(n):
+        put(
+            hout0,
+            hin0.at[j],
+            h_send.at[0, d],
+            h_recv.at[0, j],
+            {"row": lax.rem(i + d, n), "col": i},
+            None if d else i != j,
+        )
+    mid_of = low + j // per_mid
+    slot = lax.rem(j, per_mid)
+    for at, (src, dst) in enumerate(
+        ((rhs_sub.at[0, 1:, 0], rin_sub.at[slot]), (rhs_top.at[:, 0], rin_top.at[slot]))
+    ):
+        put(src, dst, r_send.at[at], r_recv.at[at, slot], {"col": mid_of}, j != mid_of)
+
+    for unit in range(pairs + topl + tpairs):
+        if unit < pairs:
+            block = lower_sub[0, unit, 0, 0]
+        elif unit < pairs + topl:
+            block = lower_link[0, unit - pairs, 0, 0]
+        else:
+            block = lower_top[unit - pairs - topl, 0, 0]
+        gate = mask[unit].astype(jnp.float32)
+        lm[unit] = (block.astype(jnp.float32) * gate).astype(jnp.bfloat16)
+
     columns = {}
-    for level in range(levels):
-        residual = rhs(level)
-        if level > 0:
-            last = level - 1
+    for level in range(1, levels):
+        last = level - 1
+        part = None
+        for b, unit in sorted(earlier_units(level)):
+            if b == last:
+                if b == 0:
+                    for c in range(n):
+                        arrived(hin0.at[c], h_recv.at[0, c])
+                    value = hin0[...].astype(jnp.float32).reshape(n * share, width)
+                    columns[b] = value.astype(jnp.bfloat16)
+                else:
+                    for q in range(mids):
+                        arrived(hin.at[b, q], h_recv.at[b, low + q])
+                    columns[b] = hin[b].reshape(n * share, width)
+            term = dot_nn(columns[b], lm[unit])
+            part = term if part is None else part + term
+        pout[level] = part.reshape(mids, wide_share, width).astype(jnp.bfloat16)
+        for q in range(mids):
+            put(
+                pout.at[level, q],
+                pin.at[level, j],
+                p_send.at[level, q],
+                p_recv.at[level, j],
+                {"col": low + q},
+                j != low + q,
+            )
+        if level == subl:
+            for t in range(topl):
+                term = part if t == 0 else dot_nn(columns[subl - 1], lm[pairs + t])
+                xout[:, t] = term.reshape(mids, wide_share, width).astype(jnp.bfloat16)
+            for q in range(mids):
+                put(
+                    xout.at[q],
+                    xin.at[j],
+                    x_send.at[q],
+                    x_recv.at[j],
+                    {"gz": 1 - g, "col": low + q},
+                )
+
+        @pl.when(is_mid)
+        def _():
+            if level == 1:
+                for at, ref in enumerate((rin_sub, rin_top)):
+                    for k in range(per_mid):
+                        arrived(ref.at[k], r_recv.at[at, k])
+            residual = rhs(level)
             for c in range(n):
-                arrived(hin.at[last, c], h_recv.at[last, c])
-            columns[last] = wide(hin.at[last])
-            part = None
-            for b, unit in earlier_units(level):
-                term = dot_nn(columns[b], lm[unit])
-                part = term if part is None else part + term
-            pout[level - 1] = part.reshape(n, share, width).astype(jnp.bfloat16)
-            for d in range(1, n):
-                c = lax.rem(j + d, n)
-                put(
-                    pout.at[level - 1, c],
-                    pin.at[level - 1, j],
-                    p_send.at[level - 1, d],
-                    p_recv.at[level - 1, j],
-                    {"col": c},
-                )
-            if level == subl:
-                for t in range(topl):
-                    term = part if t == 0 else dot_nn(columns[subl - 1], lm[pairs + t])
-                    xout[:, t] = term.reshape(n, share, width).astype(jnp.bfloat16)
-                for d in range(n):
-                    c = lax.rem(j + d, n)
-                    put(
-                        xout.at[c],
-                        xin.at[j],
-                        x_send.at[d],
-                        x_recv.at[j],
-                        {"gz": 1 - g, "col": c},
-                    )
-            residual = residual - pout[level - 1, j].astype(jnp.float32)
-            for d in range(1, n):
-                c = lax.rem(j + d, n)
-                arrived(pin.at[level - 1, c], p_recv.at[level - 1, c])
-                residual = residual - pin[level - 1, c].astype(jnp.float32)
+                arrived(pin.at[level, c], p_recv.at[level, c])
+                residual = residual - pin[level, c].astype(jnp.float32)
             if level >= subl:
                 for c in range(n):
                     if level == subl:
                         arrived(xin.at[c], x_recv.at[c])
                     residual = residual - xin[c, level - subl].astype(jnp.float32)
-        result = dot_nn(residual.astype(jnp.bfloat16), inverse(level))
-        solved[level] = result
+            result = dot_nn(residual.astype(jnp.bfloat16), inverse(level))
+            solved[level] = result
+            hout[level] = result.astype(jnp.bfloat16)
+
         if level + 1 < levels:
-            hout[level] = result.astype(jnp.bfloat16)
             for d in range(n):
                 put(
                     hout.at[level],
-                    hin.at[level, j],
+                    hin.at[level, m],
                     h_send.at[level, d],
                     h_recv.at[level, j],
                     {"row": lax.rem(i + d, n), "col": i},
                     None if d else i != j,
+                    is_mid,
                 )
 
     rows = {}
     for level in reversed(range(levels)):
-        total = solved[level]
         if level + 1 < levels:
             last = level + 1
-            for d in range(1, n):
-                c = lax.rem(j + d, n)
-                arrived(ans.at[last, c], a_recv.at[last, c])
-            rows[last] = wide(ans.at[last])
             part = None
-            for a, unit in later_units(level):
+            for a, unit in sorted(later_units(level), reverse=True):
+                if a == last:
+                    for q in range(mids):
+
+                        @pl.when(j != low + q)
+                        def _():
+                            arrived(ans.at[a, q], a_recv.at[a, q])
+
+                    rows[a] = ans[a].reshape(n * share, width)
                 term = dot_nt(rows[a], lm[unit])
                 part = term if part is None else part + term
-            qout[level] = part.reshape(n, share, width).astype(jnp.bfloat16)
-            for d in range(n):
-                c = lax.rem(j + d, n)
-                put(
-                    qout.at[level, c],
-                    qin.at[level, i],
-                    q_send.at[level, d],
-                    q_recv.at[level, i],
-                    {"row": j, "col": c},
-                    None if d else i != j,
-                )
-            for k in range(n):
-                arrived(qin.at[level, k], q_recv.at[level, k])
-                total = total - qin[level, k].astype(jnp.float32)
-        result = dot_nt(total.astype(jnp.bfloat16), inverse(level))
+            if level > 0:
+                qout[level] = part.reshape(mids, wide_share, width).astype(jnp.bfloat16)
+                for q in range(mids):
+                    put(
+                        qout.at[level, q],
+                        qin.at[level, i],
+                        q_send.at[level, q],
+                        q_recv.at[level, i],
+                        {"row": j, "col": low + q},
+                        (i != j) | (j != low + q),
+                    )
+            else:
+                qout0[...] = part.reshape(n, share, width).astype(jnp.bfloat16)
+                for d in range(n):
+                    c = lax.rem(j + d, n)
+                    put(
+                        qout0.at[c],
+                        qin0.at[i],
+                        q_send.at[0, d],
+                        q_recv.at[0, i],
+                        {"row": j, "col": c},
+                        None if d else i != j,
+                    )
+        if level == 0:
+            break
+
+        @pl.when(is_mid)
+        def _():
+            total = solved[level]
+            if level + 1 < levels:
+                for k in range(n):
+                    arrived(qin.at[level, k], q_recv.at[level, k])
+                    total = total - qin[level, k].astype(jnp.float32)
+            result = dot_nt(total.astype(jnp.bfloat16), inverse(level))
+            ans[level, m] = result.astype(jnp.bfloat16)
+            back_out[level] = result.reshape(per_mid, share, width)
+
+        for d in range(1, n):
+            put(
+                ans.at[level, m],
+                ans.at[level, m],
+                a_send.at[level, d],
+                a_recv.at[level, m],
+                {"col": lax.rem(j + d, n)},
+                None,
+                is_mid,
+            )
+        for k in range(per_mid):
+            owner = per_mid * m + k
+            put(
+                back_out.at[level, k],
+                back_in.at[level],
+                b_send.at[level, k],
+                b_recv.at[level],
+                {"col": owner},
+                owner != j,
+                is_mid,
+            )
+
+    for level in range(1, levels):
+        arrived(back_in.at[level], b_recv.at[level])
         if level < subl:
-            sol_sub[0, level, 0] = result
+            sol_sub[0, level, 0] = back_in[level]
         else:
-            sol_top[level - subl, 0] = result
-        if level > 0:
-            ans[level, j] = result.astype(jnp.bfloat16)
-            for d in range(1, n):
-                put(
-                    ans.at[level, j],
-                    ans.at[level, j],
-                    a_send.at[level, d],
-                    a_recv.at[level, j],
-                    {"col": lax.rem(j + d, n)},
-                )
-
-    for copy, remote in pending:
-        if remote is None:
+            sol_top[level - subl, 0] = back_in[level]
+    total = first[...]
+    for k in range(n):
+        arrived(qin0.at[k], q_recv.at[0, k])
+        total = total - qin0[k].astype(jnp.float32)
+    sol_sub[0, 0, 0] = dot_nt(total.astype(jnp.bfloat16), inverse(0))
+
+    for copy, goes in pending:
+        if goes is None:
             copy.wait_send()
         else:
 
-            @pl.when(remote)
+            @pl.when(goes)
             def _():
                 copy.wait_send()
 
 
 def fused_device(*args):
     rhs_sub, rhs_top, lower_sub, lower_link, lower_top = args[:5]
-    levels = rhs_sub.shape[1] + rhs_top.shape[0]
-    topl = rhs_top.shape[0]
+    subl, topl = rhs_sub.shape[1], rhs_top.shape[0]
+    levels = subl + topl
     share, width = rhs_top.shape[2:]
     n = lax.axis_size("col")
+    mids = n // 2
+    wide_share = 2 * share
     units = lower_sub.shape[1] + lower_link.shape[1] + lower_top.shape[0]
-    half, dma = jnp.bfloat16, pltpu.SemaphoreType.DMA
+    half, full, dma = jnp.bfloat16, jnp.float32, pltpu.SemaphoreType.DMA
     vmem = pl.BlockSpec(memory_space=pltpu.VMEM)
     smem = pl.BlockSpec(memory_space=pltpu.SMEM)
-    vectors = pltpu.VMEM((levels, n, share, width), half)
+
+    def buffer(dtype, *shape):
+        return pltpu.VMEM(shape + (width,), dtype)
+
+    masks = jnp.concatenate([value.reshape(-1) for value in args[7:]])
     return pl.pallas_call(
         fused_kernel,
         out_shape=(
-            jax.ShapeDtypeStruct(rhs_sub.shape, jnp.float32),
-            jax.ShapeDtypeStruct(rhs_top.shape, jnp.float32),
+            jax.ShapeDtypeStruct(rhs_sub.shape, full),
+            jax.ShapeDtypeStruct(rhs_top.shape, full),
         ),
-        in_specs=[vmem] * 7 + [smem] * 3,
+        in_specs=[vmem] * 7 + [smem],
         out_specs=(vmem, vmem),
         scratch_shapes=[
-            pltpu.VMEM((units, width, width), half),
-            pltpu.VMEM((levels, share, width), jnp.float32),
-            pltpu.VMEM((levels, share, width), half),
-            vectors,
-            vectors,
-            vectors,
-            pltpu.VMEM((n, topl, share, width), half),
-            pltpu.VMEM((n, topl, share, width), half),
-            vectors,
-            vectors,
-            vectors,
-            dma((levels, n)),
-            dma((levels, n)),
-            dma((levels, n)),
-            dma((levels, n)),
+            buffer(half, units, width),
+            buffer(full, share),
+            buffer(full, levels, wide_share),
+            buffer(half, share),
+            buffer(half, n, share),
+            buffer(half, n, share),
+            buffer(half, n, share),
+            buffer(full, 2, subl - 1, share),
+            buffer(full, 2, topl, share),
+            buffer(half, levels, wide_share),
+            buffer(half, levels, mids, wide_share),
+            buffer(half, levels, mids, wide_share),
+            buffer(half, levels, n, wide_share),
+            buffer(half, mids, topl, wide_share),
+            buffer(half, n, topl, wide_share),
+            buffer(half, levels, mids, wide_share),
+            buffer(half, levels, mids, wide_share),
+            buffer(half, levels, n, wide_share),
+            buffer(full, levels, 2, share),
+            buffer(full, levels, share),
+            dma((2,)),
+            dma((2, 2)),
+            dma((levels, n)),
+            dma((levels, n)),
+            dma((levels, n)),
+            dma((levels, n)),
+            dma((mids,)),
             dma((n,)),
-            dma((n,)),
-            dma((levels, n)),
-            dma((levels, n)),
-            dma((levels, n)),
-            dma((levels, n)),
+            dma((levels, n)),
+            dma((levels, mids)),
+            dma((levels, n)),
+            dma((levels, n)),
+            dma((levels, 2)),
+            dma((levels,)),
         ],
         compiler_params=pltpu.CompilerParams(has_side_effects=True),
-    )(*args)
+    )(*args[:7], masks)
 
 
 def choose(*args):
     rhs_top, lower_top = args[1], args[4]
-    one_each = lower_top.shape[1] == 1 and lower_top.shape[2] == 1
+    one_each = args[0].shape[1] > 1 and lower_top.shape[1] == 1 and lower_top.shape[2] == 1
     square = lax.axis_size("row") == lax.axis_size("col") and lax.axis_size("gz") == 2
-    if one_each and square and rhs_top.shape[2] % 8 == 0 and rhs_top.shape[3] % 128 == 0:
+    if one_each and square and rhs_top.shape[2] % 8 == 0 and lax.axis_size("col") % 4 == 0 and rhs_top.shape[3] % 128 == 0:
         return fused_device(*args)
     return per_device(*args)
 

time: 86 us -> 86.8 us (level)
  Pallas kernels: 81 us -> 81.9 us
    unnamed x10 -> x8, local copies, waits for them, and re-layouts: 3.46 us -> 2.81 us
where the time goes in v2:
time: 86.8 us; the launch traced here: 86.6 us
  Pallas kernels  81.9 us (94%)
  local copies, waits for them, and re-layouts  2.81 us (3%)
  between operations  1.31 us (2%)
    pallas_call x1, Pallas kernels, fused_device(): pl.pallas_call(fused_kernel, out_shape=(jax.ShapeDtypeStruct(rhs_sub.shap...  81.9 us
    unnamed x8, local copies, waits for them, and re-layouts  2.81 us

profile of v2, /device:TPU:0, one launch (start us, length us, event | category | flops | bytes accessed | tf_op | source)
XLA Modules:
  0.0 86.6 jit_solution(7848913899689936276)
XLA Ops:
  1.3 0.0 copy-start.1
  1.3 0.0 copy-start.2
  1.3 0.6 copy-done.1
  1.9 0.0 copy-done.2
  1.9 0.6 pad_add_fusion.mask
  2.5 81.9 %shard_map.113 = (f32[1,3,1,24,256]{4,3,2,1,0:T(8,128)}, f32[2,1,24,256]{3,2,1,0:T(8,128)}) custom-call(f32[1,3,1,24,256]{4,3,2,1,0:T(8,128)} %rhs_sub.1, f32[2,1,24,256]{3,2,1,0:T(8,128)} %rhs_top.1, bf16[1,3,1,1,256,256]{5,4,3,2,1,0:T(8,128)(2,1)} %lower_sub.1, bf16[1,2,1,1,256,256]{5,4,3,2,1,0:T(8,128)(2,1)} %lower_link.1, ...), custom_call_target="tpu_custom_call" | custom-call | tf_op jit(solution)/shard_map/pallas_call | solution.py:508
  84.4 0.0 copy-start
  84.4 1.5 %copy.15 = f32[1,3,1,24,256]{4,3,2,1,0:T(8,128)} copy(f32[1,3,1,24,256]{4,3,2,1,0:T(8,128)} %get-tuple-element.4) | data formatting | bytes 147456
  86.0 0.0 copy-done
  86.0 0.6 copy.16
Async XLA Ops:
  1.3 0.7 copy-start.1
  1.3 0.7 copy-start.2
  84.4 1.5 %copy-start = (f32[2,1,24,256]{3,2,1,0:T(8,128)S(1)}, f32[2,1,24,256]{3,2,1,0:T(8,128)}, u32[]{:S(2)}) copy-start(f32[2,1,24,256]{3,2,1,0:T(8,128)} %get-tuple-element.5) | copy-start | bytes 147460

commit v3 on v1

--- a/solution.py
+++ b/solution.py
@@ -183,9 +183,7 @@
     lower_top,
     inv_sub,
     inv_top,
-    mask_sub,
-    mask_link,
-    mask_top,
+    mask,
     sol_sub,
     sol_top,
     lm,
@@ -251,15 +249,16 @@
     def rhs(level):
         return rhs_sub[0, level, 0] if level < subl else rhs_top[level - subl, 0]
 
-    for unit in range(pairs + topl + tpairs):
-        if unit < pairs:
-            block, mask = lower_sub[0, unit, 0, 0], mask_sub[0, unit, 0, 0]
-        elif unit < pairs + topl:
-            block, mask = lower_link[0, unit - pairs, 0, 0], mask_link[0, unit - pairs, 0, 0]
-        else:
-            at = unit - pairs - topl
-            block, mask = lower_top[at, 0, 0], mask_top[at, 0, 0]
-        lm[unit] = (block.astype(jnp.float32) * mask.astype(jnp.float32)).astype(jnp.bfloat16)
+    def mask_blocks():
+        for unit in range(pairs + topl + tpairs):
+            if unit < pairs:
+                block = lower_sub[0, unit, 0, 0]
+            elif unit < pairs + topl:
+                block = lower_link[0, unit - pairs, 0, 0]
+            else:
+                block = lower_top[unit - pairs - topl, 0, 0]
+            gate = mask[unit].astype(jnp.float32)
+            lm[unit] = (block.astype(jnp.float32) * gate).astype(jnp.bfloat16)
 
     def earlier_units(level):
         if level < subl:
@@ -283,11 +282,12 @@
         residual = rhs(level)
         if level > 0:
             last = level - 1
-            for c in range(n):
-                arrived(hin.at[last, c], h_recv.at[last, c])
-            columns[last] = wide(hin.at[last])
             part = None
-            for b, unit in earlier_units(level):
+            for b, unit in sorted(earlier_units(level)):
+                if b == last:
+                    for c in range(n):
+                        arrived(hin.at[last, c], h_recv.at[last, c])
+                    columns[last] = wide(hin.at[last])
                 term = dot_nn(columns[b], lm[unit])
                 part = term if part is None else part + term
             pout[level - 1] = part.reshape(n, share, width).astype(jnp.bfloat16)
@@ -336,18 +336,21 @@
                     {"row": lax.rem(i + d, n), "col": i},
                     None if d else i != j,
                 )
+        if level == 0:
+            mask_blocks()
 
     rows = {}
     for level in reversed(range(levels)):
         total = solved[level]
         if level + 1 < levels:
             last = level + 1
-            for d in range(1, n):
-                c = lax.rem(j + d, n)
-                arrived(ans.at[last, c], a_recv.at[last, c])
-            rows[last] = wide(ans.at[last])
             part = None
-            for a, unit in later_units(level):
+            for a, unit in sorted(later_units(level), reverse=True):
+                if a == last:
+                    for d in range(1, n):
+                        c = lax.rem(j + d, n)
+                        arrived(ans.at[last, c], a_recv.at[last, c])
+                    rows[last] = wide(ans.at[last])
                 term = dot_nt(rows[a], lm[unit])
                 part = term if part is None else part + term
             qout[level] = part.reshape(n, share, width).astype(jnp.bfloat16)
@@ -396,6 +399,7 @@
     topl = rhs_top.shape[0]
     share, width = rhs_top.shape[2:]
     n = lax.axis_size("col")
+    masks = jnp.concatenate([value.reshape(-1) for value in args[7:]])
     units = lower_sub.shape[1] + lower_link.shape[1] + lower_top.shape[0]
     half, dma = jnp.bfloat16, pltpu.SemaphoreType.DMA
     vmem = pl.BlockSpec(memory_space=pltpu.VMEM)
@@ -407,7 +411,7 @@
             jax.ShapeDtypeStruct(rhs_sub.shape, jnp.float32),
             jax.ShapeDtypeStruct(rhs_top.shape, jnp.float32),
         ),
-        in_specs=[vmem] * 7 + [smem] * 3,
+        in_specs=[vmem] * 7 + [smem],
         out_specs=(vmem, vmem),
         scratch_shapes=[
             pltpu.VMEM((units, width, width), half),
@@ -433,7 +437,7 @@
             dma((levels, n)),
         ],
         compiler_params=pltpu.CompilerParams(has_side_effects=True),
-    )(*args)
+    )(*args[:7], masks)
 
 
 def choose(*args):

time: 86 us -> 85.9 us (level)
    unnamed x10 -> x8, local copies, waits for them, and re-layouts: 3.46 us -> 2.81 us
where the time goes in v3:
time: 85.9 us; the launch traced here: 85.7 us
  Pallas kernels  81 us (94%)
  local copies, waits for them, and re-layouts  2.81 us (3%)
  between operations  1.31 us (2%)
    pallas_call x1, Pallas kernels, fused_device(): pl.pallas_call(fused_kernel, out_shape=(jax.ShapeDtypeStruct(rhs_sub.shap...  81 us
    unnamed x8, local copies, waits for them, and re-layouts  2.81 us

profile of v3, /device:TPU:0, one launch (start us, length us, event | category | flops | bytes accessed | tf_op | source)
XLA Modules:
  0.0 85.7 jit_solution(11775120621662240131)
XLA Ops:
  1.3 0.0 copy-start.1
  1.3 0.0 copy-start.2
  1.3 0.6 copy-done.1
  1.9 0.0 copy-done.2
  1.9 0.6 pad_add_fusion.mask
  2.5 81.0 %shard_map.113 = (f32[1,3,1,24,256]{4,3,2,1,0:T(8,128)}, f32[2,1,24,256]{3,2,1,0:T(8,128)}) custom-call(f32[1,3,1,24,256]{4,3,2,1,0:T(8,128)} %rhs_sub.1, f32[2,1,24,256]{3,2,1,0:T(8,128)} %rhs_top.1, bf16[1,3,1,1,256,256]{5,4,3,2,1,0:T(8,128)(2,1)} %lower_sub.1, bf16[1,2,1,1,256,256]{5,4,3,2,1,0:T(8,128)(2,1)} %lower_link.1, ...), custom_call_target="tpu_custom_call" | custom-call | tf_op jit(solution)/shard_map/pallas_call | solution.py:408
  83.5 0.0 copy-start
  83.5 1.5 %copy.15 = f32[1,3,1,24,256]{4,3,2,1,0:T(8,128)} copy(f32[1,3,1,24,256]{4,3,2,1,0:T(8,128)} %get-tuple-element.4) | data formatting | bytes 147456
  85.0 0.0 copy-done
  85.0 0.6 copy.16
Async XLA Ops:
  1.3 0.7 copy-start.1
  1.3 0.7 copy-start.2
  83.5 1.5 %copy-start = (f32[2,1,24,256]{3,2,1,0:T(8,128)S(1)}, f32[2,1,24,256]{3,2,1,0:T(8,128)}, u32[]{:S(2)}) copy-start(f32[2,1,24,256]{3,2,1,0:T(8,128)} %get-tuple-element.5) | copy-start | bytes 147460
